TPU v7x, 256 devices: a 8x8x2 block of a 8x8x16 slice. The times are simulated.
256 devices in a mesh: groups: 2 (over z), patch: 128 (over x, y, core).
Axes of the slice: x: 8, y: 8, z: 2, core: 2. Of those that a mesh axis runs over, the one named last changes fastest.
The devices are a block of a 8x8x16 slice.
Arguments:
- nodes: bfloat16 [81920, 512], P(('groups', 'patch')), parts along dimension 0, may hold values from -6 to 6
- edges: bfloat16 [393216, 512], P(('groups', 'patch')), parts along dimension 0, may hold values from -6 to 6
- node_cot: bfloat16 [81920, 512], P(('groups', 'patch')), parts along dimension 0, may hold values from -6 to 6
- edge_cot: bfloat16 [393216, 512], P(('groups', 'patch')), parts along dimension 0, may hold values from -6 to 6
- w_edge: bfloat16 [512, 512], replicated, may hold values from -0.15625 to 0.15625
- w_send: bfloat16 [512, 512], replicated, may hold values from -0.15625 to 0.15625
- w_recv: bfloat16 [512, 512], replicated, may hold values from -0.15625 to 0.15625
- edge_bias: float32 [512], replicated, may hold values from -3 to 3
- w_edge_out: bfloat16 [512, 512], replicated, may hold values from -0.25 to 0.25
- edge_out_bias: float32 [512], replicated, may hold values from -3 to 3
- edge_gain: float32 [512], replicated, may hold values from 0.25 to 1.75
- w_node: bfloat16 [512, 512], replicated, may hold values from -0.1875 to 0.1875
- w_agg: bfloat16 [512, 512], replicated, may hold values from -0.1875 to 0.1875
- node_bias: float32 [512], replicated, may hold values from -3 to 3
- w_node_out: bfloat16 [512, 512], replicated, may hold values from -0.25 to 0.25
- node_out_bias: float32 [512], replicated, may hold values from -3 to 3
- node_gain: float32 [512], replicated, may hold values from 0.25 to 1.75
- send_slots: int32 [196608], P('patch'), may hold values from 0 to 831, as said below
- recv_slots: int32 [196608], P('patch'), may hold values from 0 to 319
- neighbour_send_lists: int32 [512, 64], P('patch'), may hold values from 0 to 319
- coarse_rows: int32 [1024], P('patch'), may hold values from 0 to 319, as said below
- far_lists: int32 [128, 128, 2], P('patch'), may hold values from 0 to 7
- block_count: int32 [128], P('patch'), may hold values from 6 to 12, as said below
Outputs:
- new_nodes: bfloat16 [81920, 512], P(('groups', 'patch')), parts along dimension 0
- new_edges: bfloat16 [393216, 512], P(('groups', 'patch')), parts along dimension 0
- node_grad: bfloat16 [81920, 512], P(('groups', 'patch')), parts along dimension 0
- edge_grad: bfloat16 [393216, 512], P(('groups', 'patch')), parts along dimension 0
There are 2 independent parts, one for each index of `groups`. A program takes and returns all parts, laid end to end along the dimension named above; an argument that names none is the same for every part. Nothing has to cross between parts.
Inputs may be any that keep to these rules, and one draw needn't show every extreme that they name: `send_slots`: addresses below 320 are rows of the edge's own patch, the next 256 are neighbour slots, the last 128 * 2 are distant slots. `coarse_rows`: the 8 rows of one patch are distinct. `block_count`: some patches have all 12 blocks live in every draw.
All inputs are finite; a program needn't handle non-finite values.
Results may differ from a plain program's by a relative error of at most 0.013.
Values may be sent and summed in bfloat16 or wider, within the bound.
A program may use at most 128 MiB of HBM per device.

v0:
```python
import functools

import jax
import jax.numpy as jnp
from jax import lax
from jax.experimental import pallas as pl
from jax.experimental.pallas import tpu as pltpu
from jax.sharding import PartitionSpec as P

BLOCK = 128
LANES = 128
MESH = pl.DeviceIdType.MESH
F32 = jnp.float32
BF16 = jnp.bfloat16
STRIDE = 75


def mm(a, b):
    return lax.dot_general(a, b, (((1,), (0,)), ((), ())), preferred_element_type=F32)


def mm_nt(a, b):
    return lax.dot_general(a, b, (((1,), (1,)), ((), ())), preferred_element_type=F32)


def mm_tn(a, b):
    return lax.dot_general(a, b, (((0,), (0,)), ((), ())), preferred_element_type=F32)


def iota(shape, dim):
    return lax.broadcasted_iota(jnp.int32, shape, dim)


def hot(mask):
    return jnp.where(mask, 1.0, 0.0).astype(BF16)


def offsets_of(count):
    return [(index // 2 + 1) * (1 - 2 * (index % 2)) for index in range(count)]


def peers_loop(peers, body):
    me = lax.axis_index("patch")

    def step(i, carry):
        body(lax.rem(me + lax.rem(i * STRIDE, peers), peers))
        return carry

    lax.fori_loop(1, peers, step, 0)


def greet_all(peers):
    barrier = pltpu.get_barrier_semaphore()

    def greet(peer):
        pl.semaphore_signal(barrier, inc=1, device_id={"patch": peer}, device_id_type=MESH)

    peers_loop(peers, greet)
    return barrier


def remote(src, dst, send, recv, peer):
    return pltpu.make_async_remote_copy(
        src_ref=src, dst_ref=dst, send_sem=send, recv_sem=recv,
        device_id={"patch": peer}, device_id_type=MESH,
    )


def spread_rows(pair, wide, packed, peers):
    parts = pair[0].shape[1] // LANES
    unit = 2 * parts
    for slot in range(2):
        for part in range(parts):
            wide[pl.ds(2 * part + slot, peers, stride=unit), :] = pair[slot][
                :, part * LANES : (part + 1) * LANES
            ]
    packed[...] = wide[...].reshape(peers, unit, LANES).astype(BF16)


def collect_rows(packed, wide, peers, width):
    parts = width // LANES
    unit = 2 * parts
    wide[...] = packed[...].astype(F32).reshape(peers * unit, LANES)
    pair = []
    for slot in range(2):
        pieces = [
            wide[pl.ds(2 * part + slot, peers, stride=unit), :] for part in range(parts)
        ]
        pair.append(jnp.concatenate(pieces, axis=1))
    return pair


def send_kernel(
    peers, nodes, near_lists, far_lists, coarse,
    table, coarse_slots,
    near_out, near_in, idx_out, idx_in, wide, far_out, far_in,
    near_send, near_recv, sems,
):
    me = lax.axis_index("patch")
    own, width = nodes.shape
    near_count, near_rows = near_lists.shape
    barrier = greet_all(peers)

    for k in range(near_count):
        mask = iota((own, near_rows), 0) == near_lists[k : k + 1, :]
        near_out[k] = mm_tn(hot(mask), nodes[...]).astype(BF16)
    wanted = far_lists[0]
    lane = iota((peers, LANES), 1)
    idx_out[...] = jnp.where(lane == 0, wanted[:, 0:1], wanted[:, 1:2]).reshape(peers, 1, LANES)

    pl.semaphore_wait(barrier, peers - 1)
    offsets = offsets_of(near_count)
    near = []
    for k in range(near_count):
        copy = remote(
            near_out.at[k], near_in.at[k], near_send.at[k], near_recv.at[k],
            lax.rem(me + offsets[k] + peers, peers),
        )
        copy.start()
        near.append(copy)
    peers_loop(
        peers,
        lambda peer: remote(
            idx_out.at[peer], idx_in.at[me], sems.at[0], sems.at[1], peer
        ).start(),
    )
    idx_in[pl.ds(me, 1)] = idx_out[pl.ds(me, 1)]
    others = pl.ds(0, peers - 1)
    remote(idx_out.at[others], idx_in.at[others], sems.at[0], sems.at[1], me).wait_recv()

    asked = idx_in[...].reshape(peers, LANES)
    slots = jnp.zeros_like(asked)
    for c in range(coarse.shape[0]):
        slots = jnp.where(asked == c, coarse[c], slots)
    coarse_slots[...] = slots
    pair = [mm(hot(iota((peers, own), 1) == slots[:, s : s + 1]), nodes[...]) for s in range(2)]
    spread_rows(pair, wide, far_out, peers)
    peers_loop(
        peers,
        lambda peer: remote(
            far_out.at[peer], far_in.at[me], sems.at[2], sems.at[3], peer
        ).start(),
    )
    far_in[pl.ds(me, 1)] = far_out[pl.ds(me, 1)]
    for copy in near:
        copy.wait_recv()
    near_total = near_count * near_rows
    table[0:near_total, :] = near_in[...].reshape(near_total, width)
    remote(far_out.at[others], far_in.at[others], sems.at[2], sems.at[3], me).wait_recv()
    pair = collect_rows(far_in, wide, peers, width)
    table[near_total : near_total + peers, :] = pair[0].astype(BF16)
    table[near_total + peers : near_total + 2 * peers, :] = pair[1].astype(BF16)
    for copy in near:
        copy.wait_send()
    remote(idx_out.at[others], idx_in.at[others], sems.at[0], sems.at[1], me).wait_send()
    remote(far_out.at[others], far_in.at[others], sems.at[2], sems.at[3], me).wait_send()


def return_kernel(
    peers, base, back, near_lists, coarse_slots,
    node_grad,
    near_out, near_in, wide, far_out, far_in, near_send, near_recv, sems,
):
    me = lax.axis_index("patch")
    own, width = base.shape
    near_count, near_rows = near_lists.shape
    near_total = near_count * near_rows
    barrier = greet_all(peers)
    near_out[...] = back[0:near_total, :].reshape(near_count, near_rows, width)
    pair = [
        back[near_total + s * peers : near_total + (s + 1) * peers, :].astype(F32)
        for s in range(2)
    ]
    spread_rows(pair, wide, far_out, peers)
    pl.semaphore_wait(barrier, peers - 1)
    offsets = offsets_of(near_count)
    near = []
    for k in range(near_count):
        copy = remote(
            near_out.at[k], near_in.at[k], near_send.at[k], near_recv.at[k],
            lax.rem(me - offsets[k] + peers, peers),
        )
        copy.start()
        near.append(copy)
    peers_loop(
        peers,
        lambda peer: remote(
            far_out.at[peer], far_in.at[me], sems.at[0], sems.at[1], peer
        ).start(),
    )
    far_in[pl.ds(me, 1)] = far_out[pl.ds(me, 1)]
    others = pl.ds(0, peers - 1)
    total = base[...]
    for k in range(near_count):
        near[k].wait_recv()
        mask = iota((own, near_rows), 0) == near_lists[k : k + 1, :]
        total = total + mm(hot(mask), near_in[k])
    slots = coarse_slots[...].T
    remote(far_out.at[others], far_in.at[others], sems.at[0], sems.at[1], me).wait_recv()
    pair = collect_rows(far_in, wide, peers, width)
    for s in range(2):
        mask = iota((own, peers), 0) == slots[s : s + 1, :]
        total = total + mm(hot(mask), pair[s].astype(BF16))
    node_grad[...] = total.astype(BF16)
    for copy in near:
        copy.wait_send()
    remote(far_out.at[others], far_in.at[others], sems.at[0], sems.at[1], me).wait_send()


def normal_stats(values):
    center = values - jnp.mean(values, axis=-1, keepdims=True)
    spread = jnp.mean(center * center, axis=-1, keepdims=True)
    inv = lax.rsqrt(spread + 1e-05)
    return center * inv, inv


def normal_back(grad, unit, inv):
    along = jnp.mean(grad * unit, axis=-1, keepdims=True)
    return inv * (grad - jnp.mean(grad, axis=-1, keepdims=True) - unit * along)


def silu_both(values):
    gate = 0.5 + 0.5 * jnp.tanh(0.5 * values)
    out = values * gate
    return out, gate + out * (1.0 - gate)


def compute_kernel(
    rows, peers, far_width,
    nodes, node_cot, table, send_rows, recv_rows, counts,
    edge_bias, edge_out_bias, edge_gain, node_bias, node_out_bias, node_gain,
    edges_h, edge_cot_h, w_edge_h, w_send_h, w_recv_h, w_edge_out_h, w_node_h, w_agg_h, w_node_out_h,
    new_nodes, base, back, new_edges_h, edge_grad_h,
    edges, edge_cot, w_edge, w_send, w_recv, w_edge_out, w_node, w_agg, w_node_out,
    new_edges, edge_grad, proj, onehot, onehot_t, slope, unit, invs, sent, dpre, dagg,
    in_sems, new_sems, grad_sems,
):
    own, width = nodes.shape
    total_edges = edges.shape[0]
    ext = table.shape[0]
    send_pad = -(-(ext + own) // LANES) * LANES
    recv_pad = -(-own // LANES) * LANES
    steps = total_edges // rows
    near_total = ext - far_width * peers

    moves = [
        (w_send_h, w_send), (w_recv_h, w_recv), (edges_h, edges), (w_edge_h, w_edge),
        (w_edge_out_h, w_edge_out), (w_agg_h, w_agg), (w_node_h, w_node),
        (w_node_out_h, w_node_out), (edge_cot_h, edge_cot),
    ]
    copies = [pltpu.make_async_copy(a, b, in_sems.at[i]) for i, (a, b) in enumerate(moves)]
    for copy in copies:
        copy.start()

    raw = send_rows[...]
    far = raw - own - near_total
    address = jnp.where(
        raw < own, raw + ext,
        jnp.where(raw < own + near_total, raw - own,
                  near_total + jnp.bitwise_and(far, 1) * peers + lax.shift_right_arithmetic(far, 1)),
    )
    target = recv_rows[...]

    groups = total_edges // LANES
    for g in range(groups):
        line = address[g : g + 1, :]
        goal = target[g : g + 1, :]
        span = slice(g * LANES, (g + 1) * LANES)
        onehot_t[0:send_pad, span] = hot(iota((send_pad, LANES), 0) == line)
        onehot_t[send_pad:, span] = hot(iota((recv_pad, LANES), 0) == goal)
        line_col = jnp.broadcast_to(line, (LANES, LANES)).T
        goal_col = jnp.broadcast_to(goal, (LANES, LANES)).T
        lane = iota((LANES, LANES), 1)
        for c in range(send_pad // LANES):
            onehot[span, c * LANES : (c + 1) * LANES] = hot(line_col == lane + c * LANES)
        for c in range(recv_pad // LANES):
            onehot[span, send_pad + c * LANES : send_pad + (c + 1) * LANES] = hot(
                goal_col == lane + c * LANES
            )

    proj[ext + own : send_pad, :] = jnp.zeros((send_pad - ext - own, width), BF16)
    proj[send_pad + own :, :] = jnp.zeros((recv_pad - own, width), BF16)
    dagg[own:, :] = jnp.zeros((recv_pad - own, width), BF16)
    copies[0].wait()
    proj[ext : ext + own, :] = mm(nodes[...], w_send[...]).astype(BF16)
    copies[1].wait()
    proj[send_pad : send_pad + own, :] = mm(nodes[...], w_recv[...]).astype(BF16)
    proj[0:ext, :] = mm(table[...], w_send[...]).astype(BF16)
    copies[2].wait()
    copies[3].wait()
    copies[4].wait()
    live_rows = counts[0] * BLOCK

    def forward(step, carry):
        at = pl.ds(pl.multiple_of(step * rows, rows), rows)
        pre = mm(edges[at, :], w_edge[...]) + mm(onehot[at, :], proj[...]) + edge_bias[...]
        hidden, rise = silu_both(pre)
        slope[at, :] = rise
        out = mm(hidden.astype(BF16), w_edge_out[...]) + edge_out_bias[...]
        normed, inv = normal_stats(out)
        unit[at, :] = normed
        invs[at, :] = jnp.broadcast_to(inv, (rows, LANES))
        alive = iota((rows, 1), 0) + step * rows < live_rows
        message = jnp.where(alive, edge_gain[...], 0.0) * normed
        sent[at, :] = message.astype(BF16)
        new_edges[at, :] = (edges[at, :].astype(F32) + message).astype(BF16)
        return carry

    lax.fori_loop(0, steps, forward, 0)
    new_copy = pltpu.make_async_copy(new_edges, new_edges_h, new_sems.at[0])

    aggregate = mm(onehot_t[send_pad : send_pad + own, :], sent[...]).astype(BF16)
    new_copy.start()
    for i in (5, 6, 7):
        copies[i].wait()
    pre = mm(nodes[...], w_node[...]) + mm(aggregate, w_agg[...]) + node_bias[...]
    hidden, rise = silu_both(pre)
    out = mm(hidden.astype(BF16), w_node_out[...]) + node_out_bias[...]
    normed, inv = normal_stats(out)
    new_nodes[...] = (nodes[...].astype(F32) + node_gain[...] * normed).astype(BF16)
    cot = node_cot[...].astype(F32)
    d_out = normal_back(node_gain[...] * cot, normed, inv).astype(BF16)
    d_pre = (mm_nt(d_out, w_node_out[...]) * rise).astype(BF16)
    dagg[0:own, :] = mm_nt(d_pre, w_agg[...]).astype(BF16)
    base[...] = cot + mm_nt(d_pre, w_node[...])
    copies[8].wait()

    def backward(step, carry):
        at = pl.ds(pl.multiple_of(step * rows, rows), rows)
        cot = edge_cot[at, :].astype(F32)
        d_message = cot + mm(onehot[at, send_pad:], dagg[...])
        alive = iota((rows, 1), 0) + step * rows < live_rows
        d_unit = jnp.where(alive, edge_gain[...], 0.0) * d_message
        d_out = normal_back(d_unit, unit[at, :], invs[at, 0:1]).astype(BF16)
        d_pre = (mm_nt(d_out, w_edge_out[...]) * slope[at, :]).astype(BF16)
        dpre[at, :] = d_pre
        edge_grad[at, :] = (cot + mm_nt(d_pre, w_edge[...])).astype(BF16)
        return carry

    lax.fori_loop(0, steps, backward, 0)
    grad_copy = pltpu.make_async_copy(edge_grad, edge_grad_h, grad_sems.at[0])

    sums = mm(onehot_t[0:ext, :], dpre[...]).astype(BF16)
    grad_copy.start()
    back[...] = mm_nt(sums, w_send[...]).astype(BF16)
    sums = mm(onehot_t[ext : ext + own, :], dpre[...]).astype(BF16)
    total = base[...] + mm_nt(sums, w_send[...])
    sums = mm(onehot_t[send_pad : send_pad + own, :], dpre[...]).astype(BF16)
    base[...] = total + mm_nt(sums, w_recv[...])
    new_copy.wait()
    grad_copy.wait()


VM = pl.BlockSpec(memory_space=pltpu.VMEM)
SM = pl.BlockSpec(memory_space=pltpu.SMEM)
ANY = pl.BlockSpec(memory_space=pl.ANY)
DMA = pltpu.SemaphoreType.DMA


def local(
    nodes, edges, node_cot, edge_cot, w_edge, w_send, w_recv, edge_bias, w_edge_out,
    edge_out_bias, edge_gain, w_node, w_agg, node_bias, w_node_out, node_out_bias, node_gain,
    send_slots, recv_slots, neighbour_send_lists, coarse_rows, far_lists, block_count,
):
    own, width = nodes.shape
    total_edges = edges.shape[0]
    peers = lax.axis_size("patch")
    near_count, near_rows = neighbour_send_lists.shape
    far_width = far_lists.shape[2]
    near_total = near_count * near_rows
    ext = near_total + far_width * peers
    unit_rows = far_width * width // LANES
    shape = jax.ShapeDtypeStruct
    exchange = [
        pltpu.VMEM((near_count, near_rows, width), BF16),
        pltpu.VMEM((near_count, near_rows, width), BF16),
    ]
    far_scratch = [
        pltpu.VMEM((peers * unit_rows, LANES), F32),
        pltpu.VMEM((peers, unit_rows, LANES), BF16),
        pltpu.VMEM((peers, unit_rows, LANES), BF16),
    ]
    table, coarse_slots = pl.pallas_call(
        functools.partial(send_kernel, peers),
        name="send_rows",
        out_shape=(shape((ext, width), BF16), shape((peers, LANES), jnp.int32)),
        in_specs=[VM, VM, VM, SM],
        out_specs=(VM, VM),
        scratch_shapes=exchange
        + [pltpu.VMEM((peers, 1, LANES), jnp.int32), pltpu.VMEM((peers, 1, LANES), jnp.int32)]
        + far_scratch
        + [DMA((near_count,)), DMA((near_count,)), DMA((4,))],
        compiler_params=pltpu.CompilerParams(collective_id=0, has_side_effects=True),
    )(nodes, neighbour_send_lists, far_lists, coarse_rows)

    rows = 256
    send_pad = -(-(ext + own) // LANES) * LANES
    recv_pad = -(-own // LANES) * LANES
    wide = lambda v: v.reshape(1, -1)
    weight = pltpu.VMEM((width, width), BF16)
    edge_b = pltpu.VMEM((total_edges, width), BF16)
    edge_f = pltpu.VMEM((total_edges, width), F32)
    new_nodes, base, back, new_edges, edge_grad = pl.pallas_call(
        functools.partial(compute_kernel, rows, peers, far_width),
        name="layer",
        out_shape=(
            shape((own, width), BF16), shape((own, width), F32), shape((ext, width), BF16),
            shape((total_edges, width), BF16), shape((total_edges, width), BF16),
        ),
        in_specs=[VM] * 5 + [SM] + [VM] * 6 + [ANY] * 9,
        out_specs=(VM, VM, VM, ANY, ANY),
        scratch_shapes=[edge_b, edge_b] + [weight] * 7
        + [
            edge_b, edge_b,
            pltpu.VMEM((send_pad + recv_pad, width), BF16),
            pltpu.VMEM((total_edges, send_pad + recv_pad), BF16),
            pltpu.VMEM((send_pad + recv_pad, total_edges), BF16),
            edge_f, edge_f,
            pltpu.VMEM((total_edges, LANES), F32),
            edge_b, edge_b,
            pltpu.VMEM((recv_pad, width), BF16),
            DMA((9,)), DMA((1,)), DMA((1,)),
        ],
        compiler_params=pltpu.CompilerParams(vmem_limit_bytes=56 << 20),
    )(
        nodes, node_cot, table, send_slots.reshape(-1, LANES), recv_slots.reshape(-1, LANES),
        block_count, wide(edge_bias), wide(edge_out_bias), wide(edge_gain), wide(node_bias),
        wide(node_out_bias), wide(node_gain),
        edges, edge_cot, w_edge, w_send, w_recv, w_edge_out, w_node, w_agg, w_node_out,
    )

    node_grad = pl.pallas_call(
        functools.partial(return_kernel, peers),
        name="return_rows",
        out_shape=shape((own, width), BF16),
        in_specs=[VM] * 4,
        out_specs=VM,
        scratch_shapes=exchange + far_scratch + [DMA((near_count,)), DMA((near_count,)), DMA((2,))],
        compiler_params=pltpu.CompilerParams(collective_id=1, has_side_effects=True),
    )(base, back, neighbour_send_lists, coarse_slots)
    return new_nodes, new_edges, node_grad, edge_grad


def solution(mesh):
    both = P(("groups", "patch"), None)
    placed = (both,) * 4 + (P(),) * 13 + (
        P("patch"), P("patch"), P("patch", None), P("patch"), P("patch", None, None), P("patch"),
    )
    return jax.shard_map(
        local, mesh=mesh, in_specs=placed, out_specs=(both,) * 4, check_vma=False
    )
```

profile of v0, /device:TPU:513, one launch (start us, length us, event | category | flops | bytes accessed | tf_op | source)
XLA Modules:
  0.0 99.8 jit_solution(1223125657500738658)
XLA Ops:
  1.3 1.4 %copy.27.far_lists = s32[1,128,2]{2,1,0:T(8,128)} copy(s32[1,128,2]{1,2,0:T(2,128)} %param.44) | data formatting | bytes 2048 | tf_op args[21]
  2.7 47.8 %send_rows.1 = (bf16[512,512]{1,0:T(8,128)(2,1)}, s32[128,128]{1,0:T(8,128)}) custom-call(bf16[320,512]{1,0:T(8,128)(2,1)} %nodes.3, s32[4,64]{1,0:T(4,128)} %near_lists.3, s32[1,128,2]{2,1,0:T(8,128)} %copy.27.far_lists, s32[8]{0:T(128)} %coarse.1), custom_call_target="tpu_custom_call" | custom-call | tf_op jit(solution)/shard_map/send_rows/pallas_call | solution.py:383
  50.5 23.4 %layer.1 = (bf16[320,512]{1,0:T(8,128)(2,1)}, f32[320,512]{1,0:T(8,128)}, bf16[512,512]{1,0:T(8,128)(2,1)}, bf16[1536,512]{1,0:T(8,128)(2,1)}, bf16[1536,512]{1,0:T(8,128)(2,1)}) custom-call(bf16[320,512]{1,0:T(8,128)(2,1)} %nodes.3, bf16[320,512]{1,0:T(8,128)(2,1)} %node_cot.1, bf16[512,512]{1,0:T(8,128)(2,1)} %get-tuple-element.11.table, ...), custom_call_target="tpu_custom_call" | custom-call | tf_op jit(solution)/shard_map/layer/pallas_call | solution.py:403
  73.9 24.2 %return_rows.1 = bf16[320,512]{1,0:T(8,128)(2,1)} custom-call(f32[320,512]{1,0:T(8,128)} %get-tuple-element.14.base, bf16[512,512]{1,0:T(8,128)(2,1)} %get-tuple-element.15.back, s32[4,64]{1,0:T(4,128)} %near_lists.3, s32[128,128]{1,0:T(8,128)} %get-tuple-element.16.coarse_slots), custom_call_target="tpu_custom_call" | custom-call | tf_op jit(solution)/shard_map/return_rows/pallas_call | solution.py:432
  98.1 1.7 %copy.30 = bf16[320,512]{1,0:T(8,128)(2,1)} copy(bf16[320,512]{1,0:T(8,128)(2,1)} %return_rows.1) | data formatting | bytes 655360
where the time goes:
time: 100 us; the launch traced here: 99.8 us
  Pallas kernels  95.3 us (95%)
  local copies, waits for them, and re-layouts  3.13 us (3%)
  between operations  1.3 us (1%)
    pallas_call x1, Pallas kernels, local(): pl.pallas_call(functools.partial(send_kernel, peers), name='send_rows', o...  47.8 us
    pallas_call x1, Pallas kernels, local(): pl.pallas_call(functools.partial(return_kernel, peers), name='return_rows...  24.2 us
    pallas_call x1, Pallas kernels, local(): pl.pallas_call(functools.partial(compute_kernel, rows, peers, far_width),...  23.4 us
    unnamed x2, local copies, waits for them, and re-layouts  3.13 us

commit v1 on v0

v1 whole, which is shorter than its diff:
```python
import functools

import jax
import jax.numpy as jnp
from jax import lax
from jax.experimental import pallas as pl
from jax.experimental.pallas import tpu as pltpu
from jax.sharding import PartitionSpec as P

BLOCK = 128
LANES = 128
MESH = pl.DeviceIdType.MESH
F32 = jnp.float32
BF16 = jnp.bfloat16
STRIDE = 75
VMEM_LIMIT = 60 << 20


def mm(a, b):
    return lax.dot_general(a, b, (((1,), (0,)), ((), ())), preferred_element_type=F32)


def mm_nt(a, b):
    return lax.dot_general(a, b, (((1,), (1,)), ((), ())), preferred_element_type=F32)


def mm_tn(a, b):
    return lax.dot_general(a, b, (((0,), (0,)), ((), ())), preferred_element_type=F32)


def iota(shape, dim):
    return lax.broadcasted_iota(jnp.int32, shape, dim)


def hot(mask):
    return jnp.where(mask, 1.0, 0.0).astype(BF16)


def offsets_of(count):
    return [(index // 2 + 1) * (1 - 2 * (index % 2)) for index in range(count)]


def peers_loop(peers, body):
    hop = STRIDE % peers

    def step(i, peer):
        peer = peer + hop
        peer = jnp.where(peer >= peers, peer - peers, peer)
        body(peer)
        return peer

    lax.fori_loop(1, peers, step, lax.axis_index("patch"))


def greet_all(peers):
    barrier = pltpu.get_barrier_semaphore()

    def greet(peer):
        pl.semaphore_signal(barrier, inc=1, device_id={"patch": peer}, device_id_type=MESH)

    peers_loop(peers, greet)
    return barrier


def remote(src, dst, send, recv, peer):
    return pltpu.make_async_remote_copy(
        src_ref=src, dst_ref=dst, send_sem=send, recv_sem=recv,
        device_id={"patch": peer}, device_id_type=MESH,
    )


def spread_rows(pair, wide, packed, peers):
    parts = pair[0].shape[1] // LANES
    unit = 2 * parts
    for slot in range(2):
        for part in range(parts):
            wide[pl.ds(2 * part + slot, peers, stride=unit), :] = pair[slot][
                :, part * LANES : (part + 1) * LANES
            ]
    packed[...] = wide[...].reshape(peers, unit, LANES).astype(BF16)


def collect_rows(packed, wide, peers, width):
    parts = width // LANES
    unit = 2 * parts
    wide[...] = packed[...].astype(F32).reshape(peers * unit, LANES)
    pair = []
    for slot in range(2):
        pieces = [
            wide[pl.ds(2 * part + slot, peers, stride=unit), :] for part in range(parts)
        ]
        pair.append(jnp.concatenate(pieces, axis=1))
    return pair


def normal_stats(values):
    center = values - jnp.mean(values, axis=-1, keepdims=True)
    spread = jnp.mean(center * center, axis=-1, keepdims=True)
    inv = lax.rsqrt(spread + 1e-05)
    return center * inv, inv


def normal_back(grad, unit, inv):
    along = jnp.mean(grad * unit, axis=-1, keepdims=True)
    return inv * (grad - jnp.mean(grad, axis=-1, keepdims=True) - unit * along)


def silu_both(values):
    gate = 0.5 + 0.5 * jnp.tanh(0.5 * values)
    out = values * gate
    return out, gate + out * (1.0 - gate)


def layer_kernel(
    rows, peers,
    coarse, counts,
    nodes_h, near_lists_h, far_lists_h, send_rows_h, recv_rows_h, node_cot_h,
    edge_bias_h, edge_out_bias_h, edge_gain_h, node_bias_h, node_out_bias_h, node_gain_h,
    edges_h, edge_cot_h, w_edge_h, w_send_h, w_recv_h, w_edge_out_h, w_node_h, w_agg_h, w_node_out_h,
    new_nodes, new_edges, node_grad, edge_grad,
    near_out, near_in, near_out_b, near_in_b, idx_out, idx_in, wide,
    far_out, far_in, far_out_b, far_in_b,
    nodes, near_lists, far_lists, send_rows, recv_rows, node_cot,
    edge_bias, edge_out_bias, edge_gain, node_bias, node_out_bias, node_gain,
    edges, edge_cot, w_edge, w_send, w_recv, w_edge_out, w_node, w_agg, w_node_out,
    proj, onehot, onehot_t, slope, unit, invs, sent, dpre, dagg,
    near_send, near_recv, near_send_b, near_recv_b, sems, in_sems,
):
    me = lax.axis_index("patch")
    own, width = nodes.shape
    total_edges = edges.shape[0]
    near_count, near_rows = near_lists.shape
    near_total = near_count * near_rows
    ext = near_total + 2 * peers
    send_pad = -(-(ext + own) // LANES) * LANES
    recv_pad = -(-own // LANES) * LANES
    steps = total_edges // rows
    offsets = offsets_of(near_count)
    others = pl.ds(0, peers - 1)

    barrier = greet_all(peers)
    moves = [
        (nodes_h, nodes), (near_lists_h, near_lists), (far_lists_h, far_lists),
        (send_rows_h, send_rows), (recv_rows_h, recv_rows), (edge_bias_h, edge_bias),
        (edge_out_bias_h, edge_out_bias), (edge_gain_h, edge_gain), (node_bias_h, node_bias),
        (node_out_bias_h, node_out_bias), (node_gain_h, node_gain), (node_cot_h, node_cot),
        (w_send_h, w_send), (w_recv_h, w_recv), (edges_h, edges), (w_edge_h, w_edge),
        (w_edge_out_h, w_edge_out), (w_agg_h, w_agg), (w_node_h, w_node),
        (w_node_out_h, w_node_out), (edge_cot_h, edge_cot),
    ]
    copies = [pltpu.make_async_copy(a, b, in_sems.at[i]) for i, (a, b) in enumerate(moves)]
    for copy in copies:
        copy.start()
    first_big = len(copies) - 9

    for i in range(3):
        copies[i].wait()
    for k in range(near_count):
        mask = iota((own, near_rows), 0) == near_lists[k : k + 1, :]
        near_out[k] = mm_tn(hot(mask), nodes[...]).astype(BF16)
    first = jnp.broadcast_to(far_lists[0, 0:1, :], (LANES, peers))
    second = jnp.broadcast_to(far_lists[0, 1:2, :], (LANES, peers))
    wanted = jnp.where(iota((LANES, peers), 0) == 0, first, second).T
    idx_out[...] = wanted.reshape(peers, 1, LANES)

    pl.semaphore_wait(barrier, peers - 1)
    peers_loop(
        peers,
        lambda peer: remote(
            idx_out.at[peer], idx_in.at[me], sems.at[0], sems.at[1], peer
        ).start(),
    )
    near = []
    for k in range(near_count):
        copy = remote(
            near_out.at[k], near_in.at[k], near_send.at[k], near_recv.at[k],
            lax.rem(me + offsets[k] + peers, peers),
        )
        copy.start()
        near.append(copy)
    idx_in[pl.ds(me, 1)] = idx_out[pl.ds(me, 1)]

    for i in range(3, first_big):
        copies[i].wait()
    copies = copies[first_big:]
    raw = send_rows[...]
    far = raw - own - near_total
    address = jnp.where(
        raw < own, raw + ext,
        jnp.where(raw < own + near_total, raw - own,
                  near_total + jnp.bitwise_and(far, 1) * peers + lax.shift_right_arithmetic(far, 1)),
    )
    target = recv_rows[...]
    lane = iota((LANES, LANES), 1)
    for g in range(total_edges // LANES):
        line = address[g : g + 1, :]
        goal = target[g : g + 1, :]
        span = slice(g * LANES, (g + 1) * LANES)
        onehot_t[0:send_pad, span] = hot(iota((send_pad, LANES), 0) == line)
        onehot_t[send_pad:, span] = hot(iota((recv_pad, LANES), 0) == goal)
        line_col = jnp.broadcast_to(line, (LANES, LANES)).T
        goal_col = jnp.broadcast_to(goal, (LANES, LANES)).T
        for c in range(send_pad // LANES):
            onehot[span, c * LANES : (c + 1) * LANES] = hot(line_col == lane + c * LANES)
        for c in range(recv_pad // LANES):
            onehot[span, send_pad + c * LANES : send_pad + (c + 1) * LANES] = hot(
                goal_col == lane + c * LANES
            )
    proj[ext + own : send_pad, :] = jnp.zeros((send_pad - ext - own, width), BF16)
    proj[send_pad + own :, :] = jnp.zeros((recv_pad - own, width), BF16)
    dagg[own:, :] = jnp.zeros((recv_pad - own, width), BF16)
    copies[0].wait()
    proj[ext : ext + own, :] = mm(nodes[...], w_send[...]).astype(BF16)
    copies[1].wait()
    proj[send_pad : send_pad + own, :] = mm(nodes[...], w_recv[...]).astype(BF16)
    copies[2].wait()
    copies[3].wait()
    for copy in near:
        copy.wait_recv()
    proj[0:near_total, :] = mm(near_in[...].reshape(near_total, width), w_send[...]).astype(BF16)

    def ahead(step, carry):
        at = pl.ds(pl.multiple_of(step * rows, rows), rows)
        slope[at, :] = (
            mm(edges[at, :], w_edge[...])
            + mm(onehot[at, 0:near_total], proj[0:near_total, :])
            + mm(onehot[at, ext:], proj[ext:, :])
            + edge_bias[...]
        )
        return carry

    lax.fori_loop(0, steps, ahead, 0)

    remote(idx_out.at[others], idx_in.at[others], sems.at[0], sems.at[1], me).wait_recv()
    asked = idx_in[...].reshape(peers, LANES)
    slots = jnp.zeros_like(asked)
    for c in range(coarse.shape[0]):
        slots = jnp.where(asked == c, coarse[c], slots)
    pair = [mm(hot(iota((peers, own), 1) == slots[:, s : s + 1]), nodes[...]) for s in range(2)]
    spread_rows(pair, wide, far_out, peers)
    peers_loop(
        peers,
        lambda peer: remote(
            far_out.at[peer], far_in.at[me], sems.at[2], sems.at[3], peer
        ).start(),
    )
    far_in[pl.ds(me, 1)] = far_out[pl.ds(me, 1)]
    slots_t = slots.T
    for i in (4, 5, 6, 7, 8):
        copies[i].wait()
    node_pre = mm(nodes[...], w_node[...]) + node_bias[...]
    live_rows = counts[0] * BLOCK

    remote(far_out.at[others], far_in.at[others], sems.at[2], sems.at[3], me).wait_recv()
    pair = collect_rows(far_in, wide, peers, width)
    for s in range(2):
        proj[near_total + s * peers : near_total + (s + 1) * peers, :] = mm(
            pair[s].astype(BF16), w_send[...]
        ).astype(BF16)

    def forward(step, carry):
        at = pl.ds(pl.multiple_of(step * rows, rows), rows)
        pre = slope[at, :] + mm(onehot[at, near_total:ext], proj[near_total:ext, :])
        hidden, rise = silu_both(pre)
        slope[at, :] = rise
        out = mm(hidden.astype(BF16), w_edge_out[...]) + edge_out_bias[...]
        normed, inv = normal_stats(out)
        unit[at, :] = normed
        invs[at, :] = jnp.broadcast_to(inv, (rows, LANES))
        alive = iota((rows, 1), 0) + step * rows < live_rows
        message = jnp.where(alive, edge_gain[...], 0.0) * normed
        sent[at, :] = message.astype(BF16)
        new_edges[at, :] = (edges[at, :].astype(F32) + message).astype(BF16)
        return carry

    lax.fori_loop(0, steps, forward, 0)

    aggregate = mm(onehot_t[send_pad : send_pad + own, :], sent[...]).astype(BF16)
    pre = node_pre + mm(aggregate, w_agg[...])
    hidden, rise = silu_both(pre)
    out = mm(hidden.astype(BF16), w_node_out[...]) + node_out_bias[...]
    normed, inv = normal_stats(out)
    new_nodes[...] = (nodes[...].astype(F32) + node_gain[...] * normed).astype(BF16)
    node_back = node_cot[...].astype(F32)
    d_out = normal_back(node_gain[...] * node_back, normed, inv).astype(BF16)
    d_node = (mm_nt(d_out, w_node_out[...]) * rise).astype(BF16)
    dagg[0:own, :] = mm_nt(d_node, w_agg[...]).astype(BF16)

    def backward(step, carry):
        at = pl.ds(pl.multiple_of(step * rows, rows), rows)
        d_message = edge_cot[at, :].astype(F32) + mm(onehot[at, send_pad:], dagg[...])
        alive = iota((rows, 1), 0) + step * rows < live_rows
        d_unit = jnp.where(alive, edge_gain[...], 0.0) * d_message
        d_out = normal_back(d_unit, unit[at, :], invs[at, 0:1]).astype(BF16)
        dpre[at, :] = (mm_nt(d_out, w_edge_out[...]) * slope[at, :]).astype(BF16)
        return carry

    lax.fori_loop(0, steps, backward, 0)

    sums = mm(onehot_t[0:ext, :], dpre[...]).astype(BF16)
    back = mm_nt(sums, w_send[...])
    near_out_b[...] = back[0:near_total, :].astype(BF16).reshape(near_count, near_rows, width)
    pair = [back[near_total + s * peers : near_total + (s + 1) * peers, :] for s in range(2)]
    spread_rows(pair, wide, far_out_b, peers)
    peers_loop(
        peers,
        lambda peer: remote(
            far_out_b.at[peer], far_in_b.at[me], sems.at[4], sems.at[5], peer
        ).start(),
    )
    near_b = []
    for k in range(near_count):
        copy = remote(
            near_out_b.at[k], near_in_b.at[k], near_send_b.at[k], near_recv_b.at[k],
            lax.rem(me - offsets[k] + peers, peers),
        )
        copy.start()
        near_b.append(copy)
    far_in_b[pl.ds(me, 1)] = far_out_b[pl.ds(me, 1)]

    sums = mm(onehot_t[ext : ext + own, :], dpre[...]).astype(BF16)
    total = node_back + mm_nt(d_node, w_node[...]) + mm_nt(sums, w_send[...])
    sums = mm(onehot_t[send_pad : send_pad + own, :], dpre[...]).astype(BF16)
    total = total + mm_nt(sums, w_recv[...])

    def finish(step, carry):
        at = pl.ds(pl.multiple_of(step * rows, rows), rows)
        grad = edge_cot[at, :].astype(F32) + mm_nt(dpre[at, :], w_edge[...])
        edge_grad[at, :] = grad.astype(BF16)
        return carry

    lax.fori_loop(0, steps, finish, 0)

    for k in range(near_count):
        near_b[k].wait_recv()
        mask = iota((own, near_rows), 0) == near_lists[k : k + 1, :]
        total = total + mm(hot(mask), near_in_b[k])
    remote(far_out_b.at[others], far_in_b.at[others], sems.at[4], sems.at[5], me).wait_recv()
    pair = collect_rows(far_in_b, wide, peers, width)
    for s in range(2):
        mask = iota((own, peers), 0) == slots_t[s : s + 1, :]
        total = total + mm(hot(mask), pair[s].astype(BF16))
    node_grad[...] = total.astype(BF16)
    for copy in near:
        copy.wait_send()
    for copy in near_b:
        copy.wait_send()
    remote(idx_out.at[others], idx_in.at[others], sems.at[0], sems.at[1], me).wait_send()
    remote(far_out.at[others], far_in.at[others], sems.at[2], sems.at[3], me).wait_send()
    remote(far_out_b.at[others], far_in_b.at[others], sems.at[4], sems.at[5], me).wait_send()


def place_kernel(a, b, c, d, a_out, b_out, c_out, d_out, sems):
    pairs = ((b, b_out), (d, d_out), (a, a_out), (c, c_out))
    copies = [pltpu.make_async_copy(x, y, sems.at[i]) for i, (x, y) in enumerate(pairs)]
    for copy in copies:
        copy.start()
    for copy in copies:
        copy.wait()


VM = pl.BlockSpec(memory_space=pltpu.VMEM)
SM = pl.BlockSpec(memory_space=pltpu.SMEM)
HBM = pl.BlockSpec(memory_space=pltpu.HBM)
ANY = pl.BlockSpec(memory_space=pl.ANY)
DMA = pltpu.SemaphoreType.DMA
ROWS = 512


def local(
    nodes, edges, node_cot, edge_cot, w_edge, w_send, w_recv, edge_bias, w_edge_out,
    edge_out_bias, edge_gain, w_node, w_agg, node_bias, w_node_out, node_out_bias, node_gain,
    send_slots, recv_slots, neighbour_send_lists, coarse_rows, far_lists, block_count,
):
    own, width = nodes.shape
    total_edges = edges.shape[0]
    peers = lax.axis_size("patch")
    near_count, near_rows = neighbour_send_lists.shape
    near_total = near_count * near_rows
    ext = near_total + 2 * peers
    unit_rows = 2 * width // LANES
    send_pad = -(-(ext + own) // LANES) * LANES
    recv_pad = -(-own // LANES) * LANES
    flat = lambda v: v.reshape(1, -1)
    near_b = pltpu.VMEM((near_count, near_rows, width), BF16)
    index_b = pltpu.VMEM((peers, 1, LANES), jnp.int32)
    far_b = pltpu.VMEM((peers, unit_rows, LANES), BF16)
    node_b = pltpu.VMEM((own, width), BF16)
    slot_b = pltpu.VMEM((total_edges // LANES, LANES), jnp.int32)
    weight = pltpu.VMEM((width, width), BF16)
    edge_b = pltpu.VMEM((total_edges, width), BF16)
    edge_f = pltpu.VMEM((total_edges, width), F32)
    shapes = tuple(
        jax.ShapeDtypeStruct((n, width), BF16) for n in (own, total_edges, own, total_edges)
    )
    results = pl.pallas_call(
        functools.partial(layer_kernel, ROWS, peers),
        name="layer",
        out_shape=tuple(pltpu.VMEM(v.shape, v.dtype) for v in shapes),
        in_specs=[SM] * 2 + [HBM] * 21,
        out_specs=(VM,) * 4,
        scratch_shapes=[near_b] * 4 + [index_b] * 2
        + [pltpu.VMEM((peers * unit_rows, LANES), F32)] + [far_b] * 4
        + [
            node_b, pltpu.VMEM(neighbour_send_lists.shape, jnp.int32), pltpu.VMEM((1, 2, peers), jnp.int32),
            slot_b, slot_b, node_b,
        ]
        + [pltpu.VMEM((1, width), F32)] * 6
        + [edge_b] * 2 + [weight] * 7
        + [
            pltpu.VMEM((send_pad + recv_pad, width), BF16),
            pltpu.VMEM((total_edges, send_pad + recv_pad), BF16),
            pltpu.VMEM((send_pad + recv_pad, total_edges), BF16),
            edge_f, edge_f,
            pltpu.VMEM((total_edges, LANES), F32),
            edge_b, edge_b,
            pltpu.VMEM((recv_pad, width), BF16),
        ]
        + [DMA((near_count,))] * 4 + [DMA((6,)), DMA((21,))],
        compiler_params=pltpu.CompilerParams(
            collective_id=0, has_side_effects=True, vmem_limit_bytes=VMEM_LIMIT
        ),
    )(
        coarse_rows, block_count, nodes, neighbour_send_lists, far_lists.transpose(0, 2, 1),
        send_slots.reshape(-1, LANES), recv_slots.reshape(-1, LANES), node_cot,
        flat(edge_bias), flat(edge_out_bias), flat(edge_gain), flat(node_bias),
        flat(node_out_bias), flat(node_gain),
        edges, edge_cot, w_edge, w_send, w_recv, w_edge_out, w_node, w_agg, w_node_out,
    )
    return pl.pallas_call(
        place_kernel,
        name="place",
        out_shape=shapes,
        in_specs=[VM] * 4,
        out_specs=(ANY,) * 4,
        scratch_shapes=[DMA((4,))],
        compiler_params=pltpu.CompilerParams(vmem_limit_bytes=8 << 20),
    )(*results)


def solution(mesh):
    both = P(("groups", "patch"), None)
    placed = (both,) * 4 + (P(),) * 13 + (
        P("patch"), P("patch"), P("patch", None), P("patch"), P("patch", None, None), P("patch"),
    )
    return jax.shard_map(
        local, mesh=mesh, in_specs=placed, out_specs=(both,) * 4, check_vma=False
    )
```

time: 100 us -> 75.9 us (0.76)
  Pallas kernels: 95.3 us -> 74.5 us
  local copies, waits for them, and re-layouts: 3.13 us -> 0 us
    pallas_call x3 -> x2, Pallas kernels: 95.3 us -> 74.5 us  [the longest x1 72.5 us: local(): pl.pallas_call(functools.partial(layer_kernel, ROWS, peers), name='layer'...]
    unnamed x2 -> x0, local copies, waits for them, and re-layouts: 3.13 us -> none
where the time goes in v1:
time: 75.9 us; the launch traced here: 75.7 us
  Pallas kernels  74.5 us (98%)
  between operations  1.3 us (2%)
    pallas_call x1, Pallas kernels, local(): pl.pallas_call(functools.partial(layer_kernel, ROWS, peers), name='layer'...  72.5 us
    pallas_call x1, Pallas kernels, local(): pl.pallas_call(place_kernel, name='place', out_shape=shapes, in_specs=[VM...  1.91 us

profile of v1, /device:TPU:513, one launch (start us, length us, event | category | flops | bytes accessed | tf_op | source)
XLA Modules:
  0.0 75.7 jit_solution(6083772126244838318)
XLA Ops:
  1.3 72.5 %layer.1 = (bf16[320,512]{1,0:T(8,128)(2,1)S(1)}, bf16[1536,512]{1,0:T(8,128)(2,1)S(1)}, bf16[320,512]{1,0:T(8,128)(2,1)S(1)}, bf16[1536,512]{1,0:T(8,128)(2,1)S(1)}) custom-call(s32[8]{0:T(128)} %coarse.1, s32[1]{0:T(128)S(6)} %copy.27.counts, bf16[320,512]{1,0:T(8,128)(2,1)} %nodes_h.1, s32[4,64]{1,0:T(4,128)} %near_lists_h.1, s32[1,2,128]{2,1,0:T(2,128)} %bitcast.17, ...), custom_call_target="tpu_custom_call" | custom-call | tf_op jit(solution)/shard_map/layer/pallas_call | solution.py:396
  73.8 1.9 %place.1 = (bf16[320,512]{1,0:T(8,128)(2,1)}, bf16[1536,512]{1,0:T(8,128)(2,1)}, bf16[320,512]{1,0:T(8,128)(2,1)}, bf16[1536,512]{1,0:T(8,128)(2,1)}) custom-call(bf16[320,512]{1,0:T(8,128)(2,1)S(1)} %get-tuple-element.8.a, bf16[1536,512]{1,0:T(8,128)(2,1)S(1)} %get-tuple-element.9.b, bf16[320,512]{1,0:T(8,128)(2,1)S(1)} %get-tuple-element.10.c, ...), custom_call_target="tpu_custom_call" | custom-call | tf_op jit(solution)/shard_map/place/pallas_call | solution.py:430

commit v2 on v1

--- a/solution.py
+++ b/solution.py
@@ -1,4 +1,5 @@
 import functools
+import math
 
 import jax
 import jax.numpy as jnp
@@ -12,7 +13,6 @@
 MESH = pl.DeviceIdType.MESH
 F32 = jnp.float32
 BF16 = jnp.bfloat16
-STRIDE = 75
 VMEM_LIMIT = 60 << 20
 
 
@@ -40,26 +40,41 @@
     return [(index // 2 + 1) * (1 - 2 * (index % 2)) for index in range(count)]
 
 
-def peers_loop(peers, body):
-    hop = STRIDE % peers
-
-    def step(i, peer):
-        peer = peer + hop
-        peer = jnp.where(peer >= peers, peer - peers, peer)
-        body(peer)
-        return peer
-
-    lax.fori_loop(1, peers, step, lax.axis_index("patch"))
-
-
-def greet_all(peers):
-    barrier = pltpu.get_barrier_semaphore()
-
-    def greet(peer):
-        pl.semaphore_signal(barrier, inc=1, device_id={"patch": peer}, device_id_type=MESH)
-
-    peers_loop(peers, greet)
-    return barrier
+def side_of(peers):
+    return math.isqrt(peers // 2)
+
+
+def far_first(side):
+    half = side // 2
+    return sorted(range(1, side), key=lambda k: -min(k, side - k)) if half else []
+
+
+def place_of(me, side):
+    core = lax.rem(me, 2)
+    line = lax.rem(lax.div(me, 2), side)
+    return lax.div(me, 2 * side), line, core
+
+
+def wrapped(value, side):
+    return jnp.where(value >= side, value - side, value)
+
+
+def every_peer(me, side, body):
+    x, y, core = place_of(me, side)
+    within = [(oy, oc) for oy in far_first(side) + [0] for oc in (0, 1)]
+    lines = {oy: 2 * wrapped(y + oy, side) for oy in range(side)}
+    cores = (core, 1 - core)
+
+    def step(i, carry):
+        away = lax.div(i + 1, 2) * (1 - 2 * lax.rem(i, 2))
+        row = wrapped(x + side // 2 + away, side) * (2 * side)
+        for oy, oc in within:
+            body(row + lines[oy] + cores[oc])
+        return carry
+
+    lax.fori_loop(0, side - 1, step, 0)
+    for oy, oc in within[:-2] + [(0, 1)]:
+        body(x * (2 * side) + lines[oy] + cores[oc])
 
 
 def remote(src, dst, send, recv, peer):
@@ -118,13 +133,13 @@
     edge_bias_h, edge_out_bias_h, edge_gain_h, node_bias_h, node_out_bias_h, node_gain_h,
     edges_h, edge_cot_h, w_edge_h, w_send_h, w_recv_h, w_edge_out_h, w_node_h, w_agg_h, w_node_out_h,
     new_nodes, new_edges, node_grad, edge_grad,
-    near_out, near_in, near_out_b, near_in_b, idx_out, idx_in, wide,
-    far_out, far_in, far_out_b, far_in_b,
+    near_out, near_in, near_out_b, near_in_b, wide, far_out_b, far_in_b,
+    row1, row2, row3, idx1, idx2, idx3, picks,
     nodes, near_lists, far_lists, send_rows, recv_rows, node_cot,
     edge_bias, edge_out_bias, edge_gain, node_bias, node_out_bias, node_gain,
     edges, edge_cot, w_edge, w_send, w_recv, w_edge_out, w_node, w_agg, w_node_out,
     proj, onehot, onehot_t, slope, unit, invs, sent, dpre, dagg,
-    near_send, near_recv, near_send_b, near_recv_b, sems, in_sems,
+    near_send, near_recv, near_send_b, near_recv_b, sems, hop_sems, in_sems,
 ):
     me = lax.axis_index("patch")
     own, width = nodes.shape
@@ -138,7 +153,21 @@
     offsets = offsets_of(near_count)
     others = pl.ds(0, peers - 1)
 
-    barrier = greet_all(peers)
+    side = side_of(peers)
+    x, y, core = place_of(me, side)
+    first_step = jnp.where(core == 0, 2 * side, 2)
+    second_step = jnp.where(core == 0, 2, 2 * side)
+    first_at = jnp.where(core == 0, x, y)
+    second_at = jnp.where(core == 0, y, x)
+    partner = me + 1 - 2 * core
+    order = far_first(side)
+    first_peers = [me + (wrapped(first_at + k, side) - first_at) * first_step for k in order]
+    second_peers = [me + (wrapped(second_at + k, side) - second_at) * second_step for k in order]
+    near_peers = [lax.rem(me + o + peers, peers) for o in offsets]
+    barrier = pltpu.get_barrier_semaphore()
+    known = first_peers + second_peers + near_peers + [partner]
+    for peer in known:
+        pl.semaphore_signal(barrier, inc=1, device_id={"patch": peer}, device_id_type=MESH)
     moves = [
         (nodes_h, nodes), (near_lists_h, near_lists), (far_lists_h, far_lists),
         (send_rows_h, send_rows), (recv_rows_h, recv_rows), (edge_bias_h, edge_bias),
@@ -155,30 +184,29 @@
 
     for i in range(3):
         copies[i].wait()
+    coarse_count = coarse.shape[0]
+    chosen = jnp.zeros((coarse_count, own), jnp.int32)
+    for c in range(coarse_count):
+        chosen = jnp.where(iota(chosen.shape, 0) == c, coarse[c], chosen)
+    rows_out = mm(hot(iota(chosen.shape, 1) == chosen), nodes[...]).astype(BF16)
+    row1[pl.ds(first_at, 1)] = rows_out.reshape(1, coarse_count, width)
+    idx1[pl.ds(first_at, 1)] = far_lists[...]
+
+    pl.semaphore_wait(barrier, len(known))
+    mine = row1.at[first_at]
+    for peer in first_peers:
+        remote(mine, mine, sems.at[0], sems.at[1], peer).start()
     for k in range(near_count):
         mask = iota((own, near_rows), 0) == near_lists[k : k + 1, :]
         near_out[k] = mm_tn(hot(mask), nodes[...]).astype(BF16)
-    first = jnp.broadcast_to(far_lists[0, 0:1, :], (LANES, peers))
-    second = jnp.broadcast_to(far_lists[0, 1:2, :], (LANES, peers))
-    wanted = jnp.where(iota((LANES, peers), 0) == 0, first, second).T
-    idx_out[...] = wanted.reshape(peers, 1, LANES)
-
-    pl.semaphore_wait(barrier, peers - 1)
-    peers_loop(
-        peers,
-        lambda peer: remote(
-            idx_out.at[peer], idx_in.at[me], sems.at[0], sems.at[1], peer
-        ).start(),
-    )
     near = []
     for k in range(near_count):
-        copy = remote(
-            near_out.at[k], near_in.at[k], near_send.at[k], near_recv.at[k],
-            lax.rem(me + offsets[k] + peers, peers),
-        )
+        copy = remote(near_out.at[k], near_in.at[k], near_send.at[k], near_recv.at[k], near_peers[k])
         copy.start()
         near.append(copy)
-    idx_in[pl.ds(me, 1)] = idx_out[pl.ds(me, 1)]
+    mine = idx1.at[first_at]
+    for peer in first_peers:
+        remote(mine, mine, sems.at[2], sems.at[3], peer).start()
 
     for i in range(3, first_big):
         copies[i].wait()
@@ -206,6 +234,35 @@
             onehot[span, send_pad + c * LANES : send_pad + (c + 1) * LANES] = hot(
                 goal_col == lane + c * LANES
             )
+    area = side * side
+    q = iota((1, peers), 1)
+    q_core = jnp.bitwise_and(q, 1)
+    q_chip = lax.shift_right_logical(q, 1)
+    q_x = q_chip // side
+    q_y = q_chip - q_x * side
+    key = jnp.where(q_core == 0, q_y * side + q_x, q_x * side + q_y)
+    key = key + jnp.where(q_core == core, 0, area)
+    for slot in range(2):
+        spot = key * coarse_count + far_lists[0, slot : slot + 1, :]
+        spot_col = jnp.broadcast_to(spot, (LANES, peers)).T
+        picks[slot * peers : (slot + 1) * peers, :] = hot(
+            iota((peers, 2 * area * coarse_count), 1) == spot_col[:, 0:1]
+        )
+
+    fewer = pl.ds(0, side - 1)
+    remote(row1.at[fewer], row1.at[fewer], sems.at[0], sems.at[1], partner).wait_recv()
+    hops = []
+    for i, peer in enumerate(second_peers):
+        copy = remote(row1, row2.at[second_at], hop_sems.at[0, i], hop_sems.at[1, i], peer)
+        copy.start()
+        hops.append(copy)
+    remote(row1, row3.at[second_at], sems.at[4], sems.at[5], partner).start()
+    row2[pl.ds(second_at, 1)] = row1[...].reshape(1, side, coarse_count, width)
+    remote(idx1.at[fewer], idx1.at[fewer], sems.at[2], sems.at[3], partner).wait_recv()
+    for peer in second_peers:
+        remote(idx1, idx2.at[second_at], sems.at[6], sems.at[7], peer).start()
+    idx2[pl.ds(second_at, 1)] = idx1[...].reshape(1, side, 2, peers)
+
     proj[ext + own : send_pad, :] = jnp.zeros((send_pad - ext - own, width), BF16)
     proj[send_pad + own :, :] = jnp.zeros((recv_pad - own, width), BF16)
     dagg[own:, :] = jnp.zeros((recv_pad - own, width), BF16)
@@ -231,32 +288,22 @@
 
     lax.fori_loop(0, steps, ahead, 0)
 
-    remote(idx_out.at[others], idx_in.at[others], sems.at[0], sems.at[1], me).wait_recv()
-    asked = idx_in[...].reshape(peers, LANES)
-    slots = jnp.zeros_like(asked)
-    for c in range(coarse.shape[0]):
-        slots = jnp.where(asked == c, coarse[c], slots)
-    pair = [mm(hot(iota((peers, own), 1) == slots[:, s : s + 1]), nodes[...]) for s in range(2)]
-    spread_rows(pair, wide, far_out, peers)
-    peers_loop(
-        peers,
-        lambda peer: remote(
-            far_out.at[peer], far_in.at[me], sems.at[2], sems.at[3], peer
-        ).start(),
-    )
-    far_in[pl.ds(me, 1)] = far_out[pl.ds(me, 1)]
-    slots_t = slots.T
+    for i in reversed(range(len(order))):
+        hops[i].wait_recv()
+        origin = wrapped(second_at + side - order[i], side)
+        remote(row2.at[origin], row3.at[origin], sems.at[4], sems.at[5], partner).start()
+    remote(idx2.at[fewer], idx2.at[fewer], sems.at[6], sems.at[7], partner).wait_recv()
+    remote(idx2, idx3, sems.at[8], sems.at[9], partner).start()
     for i in (4, 5, 6, 7, 8):
         copies[i].wait()
     node_pre = mm(nodes[...], w_node[...]) + node_bias[...]
     live_rows = counts[0] * BLOCK
 
-    remote(far_out.at[others], far_in.at[others], sems.at[2], sems.at[3], me).wait_recv()
-    pair = collect_rows(far_in, wide, peers, width)
-    for s in range(2):
-        proj[near_total + s * peers : near_total + (s + 1) * peers, :] = mm(
-            pair[s].astype(BF16), w_send[...]
-        ).astype(BF16)
+    half = area * coarse_count
+    mine_rows = mm(picks[:, 0:half], row2[...].reshape(half, width))
+    remote(row2, row3, sems.at[4], sems.at[5], partner).wait_recv()
+    far_rows = mine_rows + mm(picks[:, half:], row3[...].reshape(half, width))
+    proj[near_total:ext, :] = mm(far_rows.astype(BF16), w_send[...]).astype(BF16)
 
     def forward(step, carry):
         at = pl.ds(pl.multiple_of(step * rows, rows), rows)
@@ -302,10 +349,10 @@
     near_out_b[...] = back[0:near_total, :].astype(BF16).reshape(near_count, near_rows, width)
     pair = [back[near_total + s * peers : near_total + (s + 1) * peers, :] for s in range(2)]
     spread_rows(pair, wide, far_out_b, peers)
-    peers_loop(
-        peers,
+    every_peer(
+        me, side,
         lambda peer: remote(
-            far_out_b.at[peer], far_in_b.at[me], sems.at[4], sems.at[5], peer
+            far_out_b.at[peer], far_in_b.at[me], sems.at[10], sems.at[11], peer
         ).start(),
     )
     near_b = []
@@ -318,6 +365,22 @@
         near_b.append(copy)
     far_in_b[pl.ds(me, 1)] = far_out_b[pl.ds(me, 1)]
 
+    remote(idx2, idx3, sems.at[8], sems.at[9], partner).wait_recv()
+    found = []
+    for part in (idx2, idx3):
+        listed = part[...].reshape(2 * area, peers)
+        found.append(
+            jnp.sum(jnp.where(iota(listed.shape, 1) == me, listed, 0), axis=1, keepdims=True)
+        )
+    found = jnp.concatenate(found, axis=0)
+    slots_t = []
+    for slot in range(2):
+        there = iota((4 * area, peers), 0) == key * 2 + slot
+        asked = jnp.sum(jnp.where(there, found, 0), axis=0, keepdims=True)
+        line = jnp.zeros_like(asked)
+        for c in range(coarse_count):
+            line = jnp.where(asked == c, coarse[c], line)
+        slots_t.append(line)
     sums = mm(onehot_t[ext : ext + own, :], dpre[...]).astype(BF16)
     total = node_back + mm_nt(d_node, w_node[...]) + mm_nt(sums, w_send[...])
     sums = mm(onehot_t[send_pad : send_pad + own, :], dpre[...]).astype(BF16)
@@ -335,19 +398,24 @@
         near_b[k].wait_recv()
         mask = iota((own, near_rows), 0) == near_lists[k : k + 1, :]
         total = total + mm(hot(mask), near_in_b[k])
-    remote(far_out_b.at[others], far_in_b.at[others], sems.at[4], sems.at[5], me).wait_recv()
+    remote(far_out_b.at[others], far_in_b.at[others], sems.at[10], sems.at[11], partner).wait_recv()
     pair = collect_rows(far_in_b, wide, peers, width)
     for s in range(2):
-        mask = iota((own, peers), 0) == slots_t[s : s + 1, :]
+        mask = iota((own, peers), 0) == slots_t[s]
         total = total + mm(hot(mask), pair[s].astype(BF16))
     node_grad[...] = total.astype(BF16)
     for copy in near:
         copy.wait_send()
     for copy in near_b:
         copy.wait_send()
-    remote(idx_out.at[others], idx_in.at[others], sems.at[0], sems.at[1], me).wait_send()
-    remote(far_out.at[others], far_in.at[others], sems.at[2], sems.at[3], me).wait_send()
-    remote(far_out_b.at[others], far_in_b.at[others], sems.at[4], sems.at[5], me).wait_send()
+    remote(row1.at[fewer], row1.at[fewer], sems.at[0], sems.at[1], partner).wait_send()
+    remote(idx1.at[fewer], idx1.at[fewer], sems.at[2], sems.at[3], partner).wait_send()
+    for copy in hops:
+        copy.wait_send()
+    remote(row2, row3, sems.at[4], sems.at[5], partner).wait_send()
+    remote(idx2.at[fewer], idx2.at[fewer], sems.at[6], sems.at[7], partner).wait_send()
+    remote(idx2, idx3, sems.at[8], sems.at[9], partner).wait_send()
+    remote(far_out_b.at[others], far_in_b.at[others], sems.at[10], sems.at[11], partner).wait_send()
 
 
 def place_kernel(a, b, c, d, a_out, b_out, c_out, d_out, sems):
@@ -383,7 +451,7 @@
     recv_pad = -(-own // LANES) * LANES
     flat = lambda v: v.reshape(1, -1)
     near_b = pltpu.VMEM((near_count, near_rows, width), BF16)
-    index_b = pltpu.VMEM((peers, 1, LANES), jnp.int32)
+    side, coarse = side_of(peers), coarse_rows.shape[0]
     far_b = pltpu.VMEM((peers, unit_rows, LANES), BF16)
     node_b = pltpu.VMEM((own, width), BF16)
     slot_b = pltpu.VMEM((total_edges // LANES, LANES), jnp.int32)
@@ -399,8 +467,17 @@
         out_shape=tuple(pltpu.VMEM(v.shape, v.dtype) for v in shapes),
         in_specs=[SM] * 2 + [HBM] * 21,
         out_specs=(VM,) * 4,
-        scratch_shapes=[near_b] * 4 + [index_b] * 2
-        + [pltpu.VMEM((peers * unit_rows, LANES), F32)] + [far_b] * 4
+        scratch_shapes=[near_b] * 4
+        + [pltpu.VMEM((peers * unit_rows, LANES), F32)] + [far_b] * 2
+        + [
+            pltpu.VMEM((side, coarse, width), BF16),
+            pltpu.VMEM((side, side, coarse, width), BF16),
+            pltpu.VMEM((side, side, coarse, width), BF16),
+            pltpu.VMEM((side, 2, peers), jnp.int32),
+            pltpu.VMEM((side, side, 2, peers), jnp.int32),
+            pltpu.VMEM((side, side, 2, peers), jnp.int32),
+            pltpu.VMEM((2 * peers, 2 * side * side * coarse), BF16),
+        ]
         + [
             node_b, pltpu.VMEM(neighbour_send_lists.shape, jnp.int32), pltpu.VMEM((1, 2, peers), jnp.int32),
             slot_b, slot_b, node_b,
@@ -416,7 +493,7 @@
             edge_b, edge_b,
             pltpu.VMEM((recv_pad, width), BF16),
         ]
-        + [DMA((near_count,))] * 4 + [DMA((6,)), DMA((21,))],
+        + [DMA((near_count,))] * 4 + [DMA((12,)), DMA((2, side - 1)), DMA((21,))],
         compiler_params=pltpu.CompilerParams(
             collective_id=0, has_side_effects=True, vmem_limit_bytes=VMEM_LIMIT
         ),

time: 75.9 us -> 65.7 us (0.87)
  Pallas kernels: 74.5 us -> 64.2 us
    pallas_call x1, Pallas kernels: 72.5 us -> 62.3 us  [local(): pl.pallas_call(functools.partial(layer_kernel, ROWS, peers), name='layer'...]
where the time goes in v2:
time: 65.7 us; the launch traced here: 65.6 us
  Pallas kernels  64.2 us (98%)
  between operations  1.46 us (2%)
    pallas_call x1, Pallas kernels, local(): pl.pallas_call(functools.partial(layer_kernel, ROWS, peers), name='layer'...  62.3 us
    pallas_call x1, Pallas kernels, local(): pl.pallas_call(place_kernel, name='place', out_shape=shapes, in_specs=[VM...  1.91 us

profile of v2, /device:TPU:513, one launch (start us, length us, event | category | flops | bytes accessed | tf_op | source)
XLA Modules:
  0.0 65.6 jit_solution(11853664984513893359)
XLA Ops:
  1.3 62.3 %layer.1 = (bf16[320,512]{1,0:T(8,128)(2,1)S(1)}, bf16[1536,512]{1,0:T(8,128)(2,1)S(1)}, bf16[320,512]{1,0:T(8,128)(2,1)S(1)}, bf16[1536,512]{1,0:T(8,128)(2,1)S(1)}) custom-call(s32[8]{0:T(128)} %coarse.1, s32[1]{0:T(128)S(6)} %copy.27.counts, bf16[320,512]{1,0:T(8,128)(2,1)} %nodes_h.1, s32[4,64]{1,0:T(4,128)} %near_lists_h.1, s32[1,2,128]{2,1,0:T(2,128)} %bitcast.17, ...), custom_call_target="tpu_custom_call" | custom-call | tf_op jit(solution)/shard_map/layer/pallas_call | solution.py:464
  63.5 1.9 %place.1 = (bf16[320,512]{1,0:T(8,128)(2,1)}, bf16[1536,512]{1,0:T(8,128)(2,1)}, bf16[320,512]{1,0:T(8,128)(2,1)}, bf16[1536,512]{1,0:T(8,128)(2,1)}) custom-call(bf16[320,512]{1,0:T(8,128)(2,1)S(1)} %get-tuple-element.8.a, bf16[1536,512]{1,0:T(8,128)(2,1)S(1)} %get-tuple-element.9.b, bf16[320,512]{1,0:T(8,128)(2,1)S(1)} %get-tuple-element.10.c, ...), custom_call_target="tpu_custom_call" | custom-call | tf_op jit(solution)/shard_map/place/pallas_call | solution.py:507

commit v3 on v2

--- a/solution.py
+++ b/solution.py
@@ -120,24 +120,25 @@
     return inv * (grad - jnp.mean(grad, axis=-1, keepdims=True) - unit * along)
 
 
-def silu_both(values):
-    gate = 0.5 + 0.5 * jnp.tanh(0.5 * values)
-    out = values * gate
-    return out, gate + out * (1.0 - gate)
+def silu_both(half):
+    t = jnp.tanh(half)
+    out = half + half * t
+    return out, (1.0 + t) + out * (1.0 - t)
 
 
 def layer_kernel(
     rows, peers,
-    coarse, counts,
-    nodes_h, near_lists_h, far_lists_h, send_rows_h, recv_rows_h, node_cot_h,
+    counts,
+    nodes_h, near_lists_h, far_lists_h, coarse_h, send_rows_h, recv_rows_h, node_cot_h,
     edge_bias_h, edge_out_bias_h, edge_gain_h, node_bias_h, node_out_bias_h, node_gain_h,
     edges_h, edge_cot_h, w_edge_h, w_send_h, w_recv_h, w_edge_out_h, w_node_h, w_agg_h, w_node_out_h,
     new_nodes, new_edges, node_grad, edge_grad,
     near_out, near_in, near_out_b, near_in_b, wide, far_out_b, far_in_b,
     row1, row2, row3, idx1, idx2, idx3, picks,
-    nodes, near_lists, far_lists, send_rows, recv_rows, node_cot,
+    nodes, near_lists, far_lists, coarse, send_rows, recv_rows, node_cot,
     edge_bias, edge_out_bias, edge_gain, node_bias, node_out_bias, node_gain,
     edges, edge_cot, w_edge, w_send, w_recv, w_edge_out, w_node, w_agg, w_node_out,
+    w_edge_out_t, w_node_out_t, w_agg_t, w_send_t,
     proj, onehot, onehot_t, slope, unit, invs, sent, dpre, dagg,
     near_send, near_recv, near_send_b, near_recv_b, sems, hop_sems, in_sems,
 ):
@@ -169,7 +170,7 @@
     for peer in known:
         pl.semaphore_signal(barrier, inc=1, device_id={"patch": peer}, device_id_type=MESH)
     moves = [
-        (nodes_h, nodes), (near_lists_h, near_lists), (far_lists_h, far_lists),
+        (nodes_h, nodes), (near_lists_h, near_lists), (far_lists_h, far_lists), (coarse_h, coarse),
         (send_rows_h, send_rows), (recv_rows_h, recv_rows), (edge_bias_h, edge_bias),
         (edge_out_bias_h, edge_out_bias), (edge_gain_h, edge_gain), (node_bias_h, node_bias),
         (node_out_bias_h, node_out_bias), (node_gain_h, node_gain), (node_cot_h, node_cot),
@@ -182,7 +183,7 @@
         copy.start()
     first_big = len(copies) - 9
 
-    for i in range(3):
+    for i in range(4):
         copies[i].wait()
     coarse_count = coarse.shape[0]
     chosen = jnp.zeros((coarse_count, own), jnp.int32)
@@ -208,7 +209,7 @@
     for peer in first_peers:
         remote(mine, mine, sems.at[2], sems.at[3], peer).start()
 
-    for i in range(3, first_big):
+    for i in range(4, first_big):
         copies[i].wait()
     copies = copies[first_big:]
     raw = send_rows[...]
@@ -278,7 +279,7 @@
 
     def ahead(step, carry):
         at = pl.ds(pl.multiple_of(step * rows, rows), rows)
-        slope[at, :] = (
+        slope[at, :] = 0.5 * (
             mm(edges[at, :], w_edge[...])
             + mm(onehot[at, 0:near_total], proj[0:near_total, :])
             + mm(onehot[at, ext:], proj[ext:, :])
@@ -297,55 +298,52 @@
     for i in (4, 5, 6, 7, 8):
         copies[i].wait()
     node_pre = mm(nodes[...], w_node[...]) + node_bias[...]
+    node_back = node_cot[...].astype(F32)
+    for w, turned in ((w_edge_out, w_edge_out_t), (w_node_out, w_node_out_t), (w_agg, w_agg_t), (w_send, w_send_t)):
+        turned[...] = w[...].T
     live_rows = counts[0] * BLOCK
 
     half = area * coarse_count
     mine_rows = mm(picks[:, 0:half], row2[...].reshape(half, width))
     remote(row2, row3, sems.at[4], sems.at[5], partner).wait_recv()
     far_rows = mine_rows + mm(picks[:, half:], row3[...].reshape(half, width))
-    proj[near_total:ext, :] = mm(far_rows.astype(BF16), w_send[...]).astype(BF16)
-
-    def forward(step, carry):
-        at = pl.ds(pl.multiple_of(step * rows, rows), rows)
-        pre = slope[at, :] + mm(onehot[at, near_total:ext], proj[near_total:ext, :])
-        hidden, rise = silu_both(pre)
+    proj[near_total:ext, :] = (0.5 * mm(far_rows.astype(BF16), w_send[...])).astype(BF16)
+
+    gathered = []
+    for step in range(steps):
+        at = slice(step * rows, (step + 1) * rows)
+        half_pre = slope[at, :] + mm(onehot[at, near_total:ext], proj[near_total:ext, :])
+        hidden, rise = silu_both(half_pre)
         slope[at, :] = rise
         out = mm(hidden.astype(BF16), w_edge_out[...]) + edge_out_bias[...]
-        normed, inv = normal_stats(out)
+        center = out - jnp.mean(out, axis=-1, keepdims=True)
+        inv = lax.rsqrt(jnp.mean(center * center, axis=-1, keepdims=True) + 1e-05)
+        inv = jnp.where(iota((rows, 1), 0) + step * rows < live_rows, inv, 0.0)
+        normed = center * inv
         unit[at, :] = normed
-        invs[at, :] = jnp.broadcast_to(inv, (rows, LANES))
-        alive = iota((rows, 1), 0) + step * rows < live_rows
-        message = jnp.where(alive, edge_gain[...], 0.0) * normed
-        sent[at, :] = message.astype(BF16)
-        new_edges[at, :] = (edges[at, :].astype(F32) + message).astype(BF16)
-        return carry
-
-    lax.fori_loop(0, steps, forward, 0)
-
-    aggregate = mm(onehot_t[send_pad : send_pad + own, :], sent[...]).astype(BF16)
-    pre = node_pre + mm(aggregate, w_agg[...])
-    hidden, rise = silu_both(pre)
+        invs[at, :] = jnp.broadcast_to(0.5 * inv, (rows, LANES))
+        sent[at, :] = (edge_gain[...] * normed).astype(BF16)
+        gathered.append(mm(onehot_t[send_pad : send_pad + own, at], sent[at, :]))
+
+    aggregate = sum(gathered[1:], gathered[0]).astype(BF16)
+    hidden, rise = silu_both(0.5 * (node_pre + mm(aggregate, w_agg[...])))
     out = mm(hidden.astype(BF16), w_node_out[...]) + node_out_bias[...]
     normed, inv = normal_stats(out)
     new_nodes[...] = (nodes[...].astype(F32) + node_gain[...] * normed).astype(BF16)
-    node_back = node_cot[...].astype(F32)
-    d_out = normal_back(node_gain[...] * node_back, normed, inv).astype(BF16)
-    d_node = (mm_nt(d_out, w_node_out[...]) * rise).astype(BF16)
-    dagg[0:own, :] = mm_nt(d_node, w_agg[...]).astype(BF16)
-
-    def backward(step, carry):
-        at = pl.ds(pl.multiple_of(step * rows, rows), rows)
+    d_out = normal_back(node_gain[...] * node_back, normed, 0.5 * inv).astype(BF16)
+    d_node = (mm(d_out, w_node_out_t[...]) * rise).astype(BF16)
+    dagg[0:own, :] = mm(d_node, w_agg_t[...]).astype(BF16)
+
+    gathered = []
+    for step in range(steps):
+        at = slice(step * rows, (step + 1) * rows)
         d_message = edge_cot[at, :].astype(F32) + mm(onehot[at, send_pad:], dagg[...])
-        alive = iota((rows, 1), 0) + step * rows < live_rows
-        d_unit = jnp.where(alive, edge_gain[...], 0.0) * d_message
-        d_out = normal_back(d_unit, unit[at, :], invs[at, 0:1]).astype(BF16)
-        dpre[at, :] = (mm_nt(d_out, w_edge_out[...]) * slope[at, :]).astype(BF16)
-        return carry
-
-    lax.fori_loop(0, steps, backward, 0)
-
-    sums = mm(onehot_t[0:ext, :], dpre[...]).astype(BF16)
-    back = mm_nt(sums, w_send[...])
+        d_out = normal_back(edge_gain[...] * d_message, unit[at, :], invs[at, 0:1]).astype(BF16)
+        dpre[at, :] = (mm(d_out, w_edge_out_t[...]) * slope[at, :]).astype(BF16)
+        gathered.append(mm(onehot_t[0:ext, at], dpre[at, :]))
+
+    sums = sum(gathered[1:], gathered[0]).astype(BF16)
+    back = mm(sums, w_send_t[...])
     near_out_b[...] = back[0:near_total, :].astype(BF16).reshape(near_count, near_rows, width)
     pair = [back[near_total + s * peers : near_total + (s + 1) * peers, :] for s in range(2)]
     spread_rows(pair, wide, far_out_b, peers)
@@ -382,7 +380,7 @@
             line = jnp.where(asked == c, coarse[c], line)
         slots_t.append(line)
     sums = mm(onehot_t[ext : ext + own, :], dpre[...]).astype(BF16)
-    total = node_back + mm_nt(d_node, w_node[...]) + mm_nt(sums, w_send[...])
+    total = node_back + mm_nt(d_node, w_node[...]) + mm(sums, w_send_t[...])
     sums = mm(onehot_t[send_pad : send_pad + own, :], dpre[...]).astype(BF16)
     total = total + mm_nt(sums, w_recv[...])
 
@@ -390,6 +388,7 @@
         at = pl.ds(pl.multiple_of(step * rows, rows), rows)
         grad = edge_cot[at, :].astype(F32) + mm_nt(dpre[at, :], w_edge[...])
         edge_grad[at, :] = grad.astype(BF16)
+        new_edges[at, :] = (edges[at, :].astype(F32) + edge_gain[...] * unit[at, :]).astype(BF16)
         return carry
 
     lax.fori_loop(0, steps, finish, 0)
@@ -465,7 +464,7 @@
         functools.partial(layer_kernel, ROWS, peers),
         name="layer",
         out_shape=tuple(pltpu.VMEM(v.shape, v.dtype) for v in shapes),
-        in_specs=[SM] * 2 + [HBM] * 21,
+        in_specs=[SM] + [HBM] * 22,
         out_specs=(VM,) * 4,
         scratch_shapes=[near_b] * 4
         + [pltpu.VMEM((peers * unit_rows, LANES), F32)] + [far_b] * 2
@@ -480,10 +479,10 @@
         ]
         + [
             node_b, pltpu.VMEM(neighbour_send_lists.shape, jnp.int32), pltpu.VMEM((1, 2, peers), jnp.int32),
-            slot_b, slot_b, node_b,
+            pltpu.SMEM(coarse_rows.shape, jnp.int32), slot_b, slot_b, node_b,
         ]
         + [pltpu.VMEM((1, width), F32)] * 6
-        + [edge_b] * 2 + [weight] * 7
+        + [edge_b] * 2 + [weight] * 11
         + [
             pltpu.VMEM((send_pad + recv_pad, width), BF16),
             pltpu.VMEM((total_edges, send_pad + recv_pad), BF16),
@@ -493,12 +492,12 @@
             edge_b, edge_b,
             pltpu.VMEM((recv_pad, width), BF16),
         ]
-        + [DMA((near_count,))] * 4 + [DMA((12,)), DMA((2, side - 1)), DMA((21,))],
+        + [DMA((near_count,))] * 4 + [DMA((12,)), DMA((2, side - 1)), DMA((22,))],
         compiler_params=pltpu.CompilerParams(
             collective_id=0, has_side_effects=True, vmem_limit_bytes=VMEM_LIMIT
         ),
     )(
-        coarse_rows, block_count, nodes, neighbour_send_lists, far_lists.transpose(0, 2, 1),
+        block_count, nodes, neighbour_send_lists, far_lists.transpose(0, 2, 1), coarse_rows,
         send_slots.reshape(-1, LANES), recv_slots.reshape(-1, LANES), node_cot,
         flat(edge_bias), flat(edge_out_bias), flat(edge_gain), flat(node_bias),
         flat(node_out_bias), flat(node_gain),

time: 65.7 us -> 63 us (0.959)
  Pallas kernels: 64.2 us -> 61.4 us
    pallas_call x1, Pallas kernels: 62.3 us -> 59.5 us  [local(): pl.pallas_call(functools.partial(layer_kernel, ROWS, peers), name='layer'...]
where the time goes in v3:
time: 63 us; the launch traced here: 62.9 us
  Pallas kernels  61.4 us (97%)
  between operations  1.46 us (2%)
    pallas_call x1, Pallas kernels, local(): pl.pallas_call(functools.partial(layer_kernel, ROWS, peers), name='layer'...  59.5 us
    pallas_call x1, Pallas kernels, local(): pl.pallas_call(place_kernel, name='place', out_shape=shapes, in_specs=[VM...  1.91 us

profile of v3, /device:TPU:513, one launch (start us, length us, event | category | flops | bytes accessed | tf_op | source)
XLA Modules:
  0.0 62.9 jit_solution(3454425131906271874)
XLA Ops:
  1.3 59.5 %layer.1 = (bf16[320,512]{1,0:T(8,128)(2,1)S(1)}, bf16[1536,512]{1,0:T(8,128)(2,1)S(1)}, bf16[320,512]{1,0:T(8,128)(2,1)S(1)}, bf16[1536,512]{1,0:T(8,128)(2,1)S(1)}) custom-call(s32[1]{0:T(128)S(6)} %copy.27.counts, bf16[320,512]{1,0:T(8,128)(2,1)} %nodes_h.1, s32[4,64]{1,0:T(4,128)} %near_lists_h.1, s32[1,2,128]{2,1,0:T(2,128)} %bitcast.17, s32[8]{0:T(128)} %coarse_h.1, ...), custom_call_target="tpu_custom_call" | custom-call | tf_op jit(solution)/shard_map/layer/pallas_call | solution.py:463
  60.8 1.9 %place.1 = (bf16[320,512]{1,0:T(8,128)(2,1)}, bf16[1536,512]{1,0:T(8,128)(2,1)}, bf16[320,512]{1,0:T(8,128)(2,1)}, bf16[1536,512]{1,0:T(8,128)(2,1)}) custom-call(bf16[320,512]{1,0:T(8,128)(2,1)S(1)} %get-tuple-element.8.a, bf16[1536,512]{1,0:T(8,128)(2,1)S(1)} %get-tuple-element.9.b, bf16[320,512]{1,0:T(8,128)(2,1)S(1)} %get-tuple-element.10.c, ...), custom_call_target="tpu_custom_call" | custom-call | tf_op jit(solution)/shard_map/place/pallas_call | solution.py:506

commit v4 on v3

--- a/solution.py
+++ b/solution.py
@@ -179,9 +179,9 @@
         (w_node_out_h, w_node_out), (edge_cot_h, edge_cot),
     ]
     copies = [pltpu.make_async_copy(a, b, in_sems.at[i]) for i, (a, b) in enumerate(moves)]
-    for copy in copies:
+    first_big = len(copies) - 9
+    for copy in copies[:4]:
         copy.start()
-    first_big = len(copies) - 9
 
     for i in range(4):
         copies[i].wait()
@@ -197,6 +197,8 @@
     mine = row1.at[first_at]
     for peer in first_peers:
         remote(mine, mine, sems.at[0], sems.at[1], peer).start()
+    for copy in copies[4:]:
+        copy.start()
     for k in range(near_count):
         mask = iota((own, near_rows), 0) == near_lists[k : k + 1, :]
         near_out[k] = mm_tn(hot(mask), nodes[...]).astype(BF16)
@@ -325,14 +327,20 @@
         sent[at, :] = (edge_gain[...] * normed).astype(BF16)
         gathered.append(mm(onehot_t[send_pad : send_pad + own, at], sent[at, :]))
 
-    aggregate = sum(gathered[1:], gathered[0]).astype(BF16)
-    hidden, rise = silu_both(0.5 * (node_pre + mm(aggregate, w_agg[...])))
-    out = mm(hidden.astype(BF16), w_node_out[...]) + node_out_bias[...]
-    normed, inv = normal_stats(out)
-    new_nodes[...] = (nodes[...].astype(F32) + node_gain[...] * normed).astype(BF16)
-    d_out = normal_back(node_gain[...] * node_back, normed, 0.5 * inv).astype(BF16)
-    d_node = (mm(d_out, w_node_out_t[...]) * rise).astype(BF16)
-    dagg[0:own, :] = mm(d_node, w_agg_t[...]).astype(BF16)
+    nodes_back = []
+    part = own // NODE_PARTS
+    for h in range(NODE_PARTS):
+        at = slice(h * part, (h + 1) * part)
+        aggregate = sum(g[at] for g in gathered).astype(BF16)
+        hidden, rise = silu_both(0.5 * (node_pre[at] + mm(aggregate, w_agg[...])))
+        out = mm(hidden.astype(BF16), w_node_out[...]) + node_out_bias[...]
+        normed, inv = normal_stats(out)
+        new_nodes[at, :] = (nodes[at, :].astype(F32) + node_gain[...] * normed).astype(BF16)
+        d_out = normal_back(node_gain[...] * node_back[at], normed, 0.5 * inv).astype(BF16)
+        d_node = (mm(d_out, w_node_out_t[...]) * rise).astype(BF16)
+        dagg[at, :] = mm(d_node, w_agg_t[...]).astype(BF16)
+        nodes_back.append(d_node)
+    d_node = jnp.concatenate(nodes_back, axis=0)
 
     gathered = []
     for step in range(steps):
@@ -347,12 +355,6 @@
     near_out_b[...] = back[0:near_total, :].astype(BF16).reshape(near_count, near_rows, width)
     pair = [back[near_total + s * peers : near_total + (s + 1) * peers, :] for s in range(2)]
     spread_rows(pair, wide, far_out_b, peers)
-    every_peer(
-        me, side,
-        lambda peer: remote(
-            far_out_b.at[peer], far_in_b.at[me], sems.at[10], sems.at[11], peer
-        ).start(),
-    )
     near_b = []
     for k in range(near_count):
         copy = remote(
@@ -361,6 +363,12 @@
         )
         copy.start()
         near_b.append(copy)
+    every_peer(
+        me, side,
+        lambda peer: remote(
+            far_out_b.at[peer], far_in_b.at[me], sems.at[10], sems.at[11], peer
+        ).start(),
+    )
     far_in_b[pl.ds(me, 1)] = far_out_b[pl.ds(me, 1)]
 
     remote(idx2, idx3, sems.at[8], sems.at[9], partner).wait_recv()
@@ -431,7 +439,7 @@
 HBM = pl.BlockSpec(memory_space=pltpu.HBM)
 ANY = pl.BlockSpec(memory_space=pl.ANY)
 DMA = pltpu.SemaphoreType.DMA
-ROWS = 512
+NODE_PARTS = 1
 
 
 def local(
@@ -461,7 +469,7 @@
         jax.ShapeDtypeStruct((n, width), BF16) for n in (own, total_edges, own, total_edges)
     )
     results = pl.pallas_call(
-        functools.partial(layer_kernel, ROWS, peers),
+        functools.partial(layer_kernel, total_edges, peers),
         name="layer",
         out_shape=tuple(pltpu.VMEM(v.shape, v.dtype) for v in shapes),
         in_specs=[SM] + [HBM] * 22,

time: 63 us -> 62.7 us (level)
  no operation moved by 1% of the time
where the time goes in v4:
time: 62.7 us; the launch traced here: 62.6 us
  Pallas kernels  61.1 us (97%)
  between operations  1.46 us (2%)
    pallas_call x1, Pallas kernels, local(): pl.pallas_call(functools.partial(layer_kernel, total_edges, peers), name=...  59.2 us
    pallas_call x1, Pallas kernels, local(): pl.pallas_call(place_kernel, name='place', out_shape=shapes, in_specs=[VM...  1.91 us

profile of v4, /device:TPU:513, one launch (start us, length us, event | category | flops | bytes accessed | tf_op | source)
XLA Modules:
  0.0 62.6 jit_solution(12323586908474111966)
XLA Ops:
  1.3 59.2 %layer.1 = (bf16[320,512]{1,0:T(8,128)(2,1)S(1)}, bf16[1536,512]{1,0:T(8,128)(2,1)S(1)}, bf16[320,512]{1,0:T(8,128)(2,1)S(1)}, bf16[1536,512]{1,0:T(8,128)(2,1)S(1)}) custom-call(s32[1]{0:T(128)S(6)} %copy.27.counts, bf16[320,512]{1,0:T(8,128)(2,1)} %nodes_h.1, s32[4,64]{1,0:T(4,128)} %near_lists_h.1, s32[1,2,128]{2,1,0:T(2,128)} %bitcast.17, s32[8]{0:T(128)} %coarse_h.1, ...), custom_call_target="tpu_custom_call" | custom-call | tf_op jit(solution)/shard_map/layer/pallas_call | solution.py:471
  60.5 1.9 %place.1 = (bf16[320,512]{1,0:T(8,128)(2,1)}, bf16[1536,512]{1,0:T(8,128)(2,1)}, bf16[320,512]{1,0:T(8,128)(2,1)}, bf16[1536,512]{1,0:T(8,128)(2,1)}) custom-call(bf16[320,512]{1,0:T(8,128)(2,1)S(1)} %get-tuple-element.8.a, bf16[1536,512]{1,0:T(8,128)(2,1)S(1)} %get-tuple-element.9.b, bf16[320,512]{1,0:T(8,128)(2,1)S(1)} %get-tuple-element.10.c, ...), custom_call_target="tpu_custom_call" | custom-call | tf_op jit(solution)/shard_map/place/pallas_call | solution.py:514

commit v5 on v4

--- a/solution.py
+++ b/solution.py
@@ -355,6 +355,12 @@
     near_out_b[...] = back[0:near_total, :].astype(BF16).reshape(near_count, near_rows, width)
     pair = [back[near_total + s * peers : near_total + (s + 1) * peers, :] for s in range(2)]
     spread_rows(pair, wide, far_out_b, peers)
+    every_peer(
+        me, side,
+        lambda peer: remote(
+            far_out_b.at[peer], far_in_b.at[me], sems.at[10], sems.at[11], peer
+        ).start(),
+    )
     near_b = []
     for k in range(near_count):
         copy = remote(
@@ -363,12 +369,6 @@
         )
         copy.start()
         near_b.append(copy)
-    every_peer(
-        me, side,
-        lambda peer: remote(
-            far_out_b.at[peer], far_in_b.at[me], sems.at[10], sems.at[11], peer
-        ).start(),
-    )
     far_in_b[pl.ds(me, 1)] = far_out_b[pl.ds(me, 1)]
 
     remote(idx2, idx3, sems.at[8], sems.at[9], partner).wait_recv()
@@ -401,15 +401,17 @@
 
     lax.fori_loop(0, steps, finish, 0)
 
+    near_masks = [
+        hot(iota((own, near_rows), 0) == near_lists[k : k + 1, :]) for k in range(near_count)
+    ]
+    far_masks = [hot(iota((own, peers), 0) == slots_t[s]) for s in range(2)]
     for k in range(near_count):
         near_b[k].wait_recv()
-        mask = iota((own, near_rows), 0) == near_lists[k : k + 1, :]
-        total = total + mm(hot(mask), near_in_b[k])
+        total = total + mm(near_masks[k], near_in_b[k])
     remote(far_out_b.at[others], far_in_b.at[others], sems.at[10], sems.at[11], partner).wait_recv()
     pair = collect_rows(far_in_b, wide, peers, width)
     for s in range(2):
-        mask = iota((own, peers), 0) == slots_t[s]
-        total = total + mm(hot(mask), pair[s].astype(BF16))
+        total = total + mm(far_masks[s], pair[s].astype(BF16))
     node_grad[...] = total.astype(BF16)
     for copy in near:
         copy.wait_send()
@@ -425,9 +427,18 @@
     remote(far_out_b.at[others], far_in_b.at[others], sems.at[10], sems.at[11], partner).wait_send()
 
 
+PIECES = 4
+
+
 def place_kernel(a, b, c, d, a_out, b_out, c_out, d_out, sems):
-    pairs = ((b, b_out), (d, d_out), (a, a_out), (c, c_out))
-    copies = [pltpu.make_async_copy(x, y, sems.at[i]) for i, (x, y) in enumerate(pairs)]
+    copies = []
+    for x, y in ((b, b_out), (d, d_out)):
+        rows = x.shape[0] // PIECES
+        for i in range(PIECES):
+            at = pl.ds(i * rows, rows)
+            copies.append(pltpu.make_async_copy(x.at[at], y.at[at], sems.at[len(copies)]))
+    for x, y in ((a, a_out), (c, c_out)):
+        copies.append(pltpu.make_async_copy(x, y, sems.at[len(copies)]))
     for copy in copies:
         copy.start()
     for copy in copies:
@@ -517,7 +528,7 @@
         out_shape=shapes,
         in_specs=[VM] * 4,
         out_specs=(ANY,) * 4,
-        scratch_shapes=[DMA((4,))],
+        scratch_shapes=[DMA((2 * PIECES + 2,))],
         compiler_params=pltpu.CompilerParams(vmem_limit_bytes=8 << 20),
     )(*results)
 

time: 62.7 us -> 62.7 us (level)
  no operation moved by 1% of the time
where the time goes in v5:
time: 62.7 us; the launch traced here: 62.6 us
  Pallas kernels  61.1 us (97%)
  between operations  1.46 us (2%)
    pallas_call x1, Pallas kernels, local(): pl.pallas_call(functools.partial(layer_kernel, total_edges, peers), name=...  59.2 us
    pallas_call x1, Pallas kernels, local(): pl.pallas_call(place_kernel, name='place', out_shape=shapes, in_specs=[VM...  1.96 us

profile of v5, /device:TPU:513, one launch (start us, length us, event | category | flops | bytes accessed | tf_op | source)
XLA Modules:
  0.0 62.6 jit_solution(13059542209183101852)
XLA Ops:
  1.3 59.2 %layer.1 = (bf16[320,512]{1,0:T(8,128)(2,1)S(1)}, bf16[1536,512]{1,0:T(8,128)(2,1)S(1)}, bf16[320,512]{1,0:T(8,128)(2,1)S(1)}, bf16[1536,512]{1,0:T(8,128)(2,1)S(1)}) custom-call(s32[1]{0:T(128)S(6)} %copy.27.counts, bf16[320,512]{1,0:T(8,128)(2,1)} %nodes_h.1, s32[4,64]{1,0:T(4,128)} %near_lists_h.1, s32[1,2,128]{2,1,0:T(2,128)} %bitcast.17, s32[8]{0:T(128)} %coarse_h.1, ...), custom_call_target="tpu_custom_call" | custom-call | tf_op jit(solution)/shard_map/layer/pallas_call | solution.py:482
  60.5 2.0 %place.1 = (bf16[320,512]{1,0:T(8,128)(2,1)}, bf16[1536,512]{1,0:T(8,128)(2,1)}, bf16[320,512]{1,0:T(8,128)(2,1)}, bf16[1536,512]{1,0:T(8,128)(2,1)}) custom-call(bf16[320,512]{1,0:T(8,128)(2,1)S(1)} %get-tuple-element.8.a, bf16[1536,512]{1,0:T(8,128)(2,1)S(1)} %get-tuple-element.9.b, bf16[320,512]{1,0:T(8,128)(2,1)S(1)} %get-tuple-element.10.c, ...), custom_call_target="tpu_custom_call" | custom-call | tf_op jit(solution)/shard_map/place/pallas_call | solution.py:525
